TPU v7x, 32 devices: a whole 2x2x4 slice. The times are simulated.
32 devices in a mesh: front: 4 (over y, core), blk: 8 (over z, x).
Axes of the slice: x: 2, y: 2, z: 4, core: 2. Of those that a mesh axis runs over, the one named last changes fastest.
Arguments:
- front: float32 [4, 1024, 1024], P('front', 'blk'), parts along dimension 0, may hold values from -8 to 40, as said below
- child: float32 [4, 512, 512], P('front', 'blk'), parts along dimension 0, may hold values from -1 to 4, as said below
- index_map: int32 [2048], P('front'), parts along dimension 0, may hold values from 0 to 1023, as said below
Outputs:
- factored: float32 [4, 1024, 1024], P('front', 'blk'), parts along dimension 0
There are 4 independent parts, one for each index of `front`. A program takes and returns all parts, laid end to end along the dimension named above; each array names one. Nothing has to cross between parts.
Inputs may be any that keep to these rules, and one draw needn't show every extreme that they name: front is symmetric and positive definite. child is symmetric and positive semidefinite. `index_map`: tile t of the child (indices t * 64 to t * 64 + 63, with t = k * 8 + e and e < 8) maps in increasing order onto 64 different indices of the front's block column b = k * 8 + ((e + h) mod 8), where h is half of 8, that is onto indices b * 128 to b * 128 + 127; no two child indices share a front index.
All inputs are finite; a program needn't handle non-finite values.
Results may differ from a plain program's by a relative error of at most 0.0034.
Values may be sent and summed in bfloat16 or wider, within the bound.
No kernel may reach another device: no remote copies, remote signals or barrier semaphores. Data moves between devices by JAX's collectives and lax.ppermute only.
A program may use at most 128 MiB of HBM per device.

v0:
```python
import jax
import jax.numpy as jnp
from jax import lax
from jax.sharding import PartitionSpec as P

PANEL_WIDTH = 512
BLOCK_WIDTH = 128
COL_BLOCKS = 1
TILE_WIDTH = 64
HIGHEST = lax.Precision.HIGHEST


def from_behind(shard, axis, by):
    count = lax.axis_size(axis)
    return lax.ppermute(shard, axis, [(i, (i + by) % count) for i in range(count)])


def column_numbers(cycle_size, my_index):
    local_ids = jnp.arange(COL_BLOCKS * BLOCK_WIDTH, dtype=jnp.int32)
    return (
        local_ids // BLOCK_WIDTH * cycle_size + my_index
    ) * BLOCK_WIDTH + local_ids % BLOCK_WIDTH


def row_numbers(cycle_size):
    stored = jnp.arange(cycle_size * COL_BLOCKS * BLOCK_WIDTH, dtype=jnp.int32)
    holder = stored // (COL_BLOCKS * BLOCK_WIDTH)
    within = stored // BLOCK_WIDTH % COL_BLOCKS
    return (within * cycle_size + holder) * BLOCK_WIDTH + stored % BLOCK_WIDTH


def cycle_rows(matrix, cycle_size):
    height = matrix.shape[0]
    return (
        matrix.reshape(height, COL_BLOCKS, cycle_size, BLOCK_WIDTH)
        .transpose(0, 2, 1, 3)
        .reshape(height, -1)
    )


def natural_rows(matrix, cycle_size):
    height = matrix.shape[0]
    return (
        matrix.reshape(height, cycle_size, COL_BLOCKS, BLOCK_WIDTH)
        .transpose(0, 2, 1, 3)
        .reshape(height, -1)
    )


def panel_rows(matrix, row_start, cycle_size):
    first_owner = row_start // BLOCK_WIDTH
    owner_count = PANEL_WIDTH // BLOCK_WIDTH
    height = matrix.shape[0]
    blocks = matrix.reshape(height, cycle_size, COL_BLOCKS, BLOCK_WIDTH)
    return blocks[:, first_owner : first_owner + owner_count, 0, :].reshape(height, PANEL_WIDTH)


def ownership(row_start, my_index):
    first_owner = row_start // BLOCK_WIDTH
    owner_count = PANEL_WIDTH // BLOCK_WIDTH
    is_owner = (my_index >= first_owner) & (my_index < first_owner + owner_count)
    column_start = jnp.clip(my_index - first_owner, 0, owner_count - 1) * BLOCK_WIDTH
    return (is_owner, column_start)


def collect(stacked, row_start, my_index):
    is_owner, column_start = ownership(row_start, my_index)
    padded = jnp.zeros((stacked.shape[0], PANEL_WIDTH, PANEL_WIDTH), jnp.float32)
    padded = lax.dynamic_update_slice(
        padded, jnp.where(is_owner, stacked, 0.0), (0, column_start, 0)
    )
    result = lax.psum(padded, "blk")
    return result


def own_rows(diag_factor, panel_part, row_start, columns):
    solved = lax.linalg.triangular_solve(
        diag_factor, panel_part, left_side=False, lower=True, transpose_a=True
    )
    offsets = columns - row_start
    diag_rows = jnp.take(diag_factor, jnp.clip(offsets, 0, PANEL_WIDTH - 1), axis=0)
    inside = (offsets >= 0) & (offsets < PANEL_WIDTH)
    before = offsets < 0
    return jnp.where(inside[:, None], diag_rows, jnp.where(before[:, None], 0.0, solved))


def make_refresh(working, lowered, owned_panels):

    def refresh(received, offset):
        updated = working - lax.dot_general(
            lowered, received, (((1,), (1,)), ((), ())), preferred_element_type=jnp.float32
        )
        leading = updated
        for is_owner, column_start in owned_panels:
            factor_column = (
                lax.dynamic_slice_in_dim(received, column_start, BLOCK_WIDTH, 1)
                .astype(jnp.float32)
                .T
            )
            leading = jnp.where(is_owner, factor_column, leading)
        return jnp.concatenate([leading, updated[BLOCK_WIDTH:]], axis=0)

    return refresh


def assemble(front, child, index_map, cycle_size, my_index):
    half_cycle = cycle_size // 2
    arrived_tiles = from_behind(child, "blk", half_cycle)
    full_order = 2 * index_map.shape[0]
    tile_places = (index_map % BLOCK_WIDTH).reshape(COL_BLOCKS, cycle_size, TILE_WIDTH)
    places = jnp.arange(BLOCK_WIDTH, dtype=jnp.int32)
    row_table = (tile_places[..., None] == places).astype(jnp.float32)
    shaped = arrived_tiles.reshape(COL_BLOCKS, TILE_WIDTH, COL_BLOCKS, cycle_size, TILE_WIDTH)
    spread = jnp.einsum("acbei,beiq->acbeq", shaped, row_table, precision=HIGHEST)
    spread = jnp.roll(spread, half_cycle, axis=3).reshape(COL_BLOCKS, TILE_WIDTH, full_order)
    source = (my_index - half_cycle) % cycle_size
    own_places = lax.dynamic_index_in_dim(tile_places, source, axis=1, keepdims=False)
    column_table = (own_places[..., None] == places).astype(jnp.float32)
    placed = jnp.einsum("kcq,kcn->kqn", column_table, spread, precision=HIGHEST)
    return front + placed


def on_device(front, child, index_map):
    cycle_size = lax.axis_size("blk")
    my_index = lax.axis_index("blk")
    local_width = COL_BLOCKS * BLOCK_WIDTH
    assembled = assemble(front, child, index_map, cycle_size, my_index).reshape(local_width, -1)
    working = cycle_rows(assembled, cycle_size)
    columns = column_numbers(cycle_size, my_index)
    for row_start in (0, PANEL_WIDTH):
        panel_part = panel_rows(working, row_start, cycle_size)
        diag_block = collect(panel_part[None, :BLOCK_WIDTH], row_start, my_index)[0]
        lowered = own_rows(jnp.linalg.cholesky(diag_block), panel_part, row_start, columns).astype(
            jnp.bfloat16
        )
        refresh = make_refresh(working, lowered, (ownership(row_start, my_index),))
        working = refresh(lax.all_gather(lowered, "blk", axis=0, tiled=True), jnp.int32(0))
    trailing = columns >= 2 * PANEL_WIDTH
    leading_rows = row_numbers(cycle_size) < 2 * PANEL_WIDTH
    working = jnp.where(trailing[:, None] & leading_rows[None, :], 0.0, working)
    return natural_rows(working, cycle_size).reshape(COL_BLOCKS, BLOCK_WIDTH, -1)


def solution(mesh):
    placed = (P("front", "blk", None), P("front", "blk", None), P("front"))
    return jax.shard_map(
        on_device, mesh=mesh, in_specs=placed, out_specs=P("front", "blk", None), check_vma=False
    )
```

profile of v0, /device:TPU:0, one launch (start us, length us, event | category | flops | bytes accessed | tf_op | source)
XLA Modules:
  0.0 557.0 jit_solution(17881052555522516391)
XLA Ops:
  6.5 4.1 collective-permute-start
  11.5 5.7 %collective-permute-done = f32[1,64,512]{2,1,0:T(8,128)S(1)} collective-permute-done((f32[1,64,512]{2,1,0:T(8,128)}, f32[1,64,512]{2,1,0:T(8,128)S(1)}, u32[]{:S(2)}, u32[]{:S(2)}) %collective-permute-start) | collective-permute-done | bytes 131104 | tf_op jit(solution)/shard_map/ppermute | solution.py:15
  17.8 0.8 copy-done.10
  19.6 1.0 copy-done.2
  20.7 79.5 %all-reduce.4.cloned.1.call-done = f32[512,512]{0,1:T(8,128)} async-done(((f32[512,512]{0,1:T(8,128)}), f32[512,512]{0,1:T(8,128)}) %all-reduce.4.cloned.1.call-update) | async-done | bytes 1048592 | tf_op jit(solution)/shard_map/psum | solution.py:72
  100.2 1.6 copy.13
  102.1 1.0 copy-done.6
  103.1 11.7 %cholesky.286 = f32[128,128]{1,0:T(8,128)S(1)} custom-call(f32[128,128]{1,0:T(8,128)S(1)} %cholesky.426), custom_call_target="Cholesky" | custom-call | tf_op jit(solution)/shard_map/jit(cholesky)/cholesky | solution.py:133
  115.0 9.8 %custom-call.27 = f32[1,128,128]{1,2,0:T(8,128)S(1)} custom-call(f32[1,128,128]{2,1,0:T(8,128)S(1)} %get-tuple-element.73), custom_call_target="InvertDiagBlocksLowerTriangular" | custom-call | tf_op jit(solution)/shard_map/jit(cholesky)/cholesky | solution.py:133
  125.5 11.7 %cholesky.305 = f32[128,128]{1,0:T(8,128)S(1)} custom-call(f32[128,128]{1,0:T(8,128)S(1)} %cholesky.430), custom_call_target="Cholesky" | custom-call | tf_op jit(solution)/shard_map/jit(cholesky)/cholesky | solution.py:133
  137.2 10.0 %custom-call.28 = f32[1,128,128]{1,2,0:T(8,128)S(1)} custom-call(f32[1,128,128]{2,1,0:T(8,128)S(1)} %get-tuple-element.70), custom_call_target="InvertDiagBlocksLowerTriangular" | custom-call | tf_op jit(solution)/shard_map/jit(cholesky)/cholesky | solution.py:133
  148.0 11.7 %cholesky.326 = f32[128,128]{1,0:T(8,128)S(1)} custom-call(f32[128,128]{1,0:T(8,128)S(1)} %cholesky.435), custom_call_target="Cholesky" | custom-call | tf_op jit(solution)/shard_map/jit(cholesky)/cholesky | solution.py:133
  159.7 0.7 compare_reduce_fusion.5
  160.4 9.8 %custom-call.29 = f32[1,128,128]{1,2,0:T(8,128)S(1)} custom-call(f32[1,128,128]{2,1,0:T(8,128)S(1)} %get-tuple-element.67), custom_call_target="InvertDiagBlocksLowerTriangular" | custom-call | tf_op jit(solution)/shard_map/jit(cholesky)/cholesky | solution.py:133
  170.8 11.7 %cholesky.343 = f32[128,128]{1,0:T(8,128)S(1)} custom-call(f32[128,128]{1,0:T(8,128)S(1)} %convolution_subtract_fusion.13), custom_call_target="Cholesky" | custom-call | tf_op jit(solution)/shard_map/jit(cholesky)/cholesky | solution.py:133
  186.5 12.0 %fusion.8 = (f32[512,512]{1,0:T(8,128)S(1)}, bf16[512,512]{1,0:T(8,128)(2,1)S(1)}) fusion(f32[512,512]{1,0:T(8,128)S(1)} %get-tuple-element.65, pred[]{:T(512)S(6)} %cholesky.348), kind=kLoop, calls=%fused_computation.38 | loop fusion | flops 1310720 | bytes 2621441 | tf_op jit(solution)/shard_map/triangular_solve/select.3 | solution.py:77
  198.5 8.1 %while.4 = (s32[]{:T(128)}, f32[512,512]{1,0:T(8,128)S(1)}, s32[4,2]{0,1:T(2,128)S(1)}, f32[4,128,128]{2,1,0:T(8,128)S(1)}, s32[]{:T(128)}) while((s32[]{:T(128)}, f32[512,512]{1,0:T(8,128)S(1)}, s32[4,2]{0,1:T(2,128)S(1)}, f32[4,128,128]{2,1,0:T(8,128)S(1)}, s32[]{:T(128)}) %tuple.61), condition=%wide.while_cond, body=%wide.while_body.sunk | while | flops 2 | bytes 131181 | solution.py:77
  199.1 1.3 bitcast_dynamic-update-slice_fusion.4
  201.2 1.3 bitcast_dynamic-update-slice_fusion.4
  203.2 1.3 bitcast_dynamic-update-slice_fusion.4
  205.3 1.3 bitcast_dynamic-update-slice_fusion.4
  206.6 39.3 %custom-call.30 = f32[4,128,128]{1,2,0:T(8,128)S(1)} custom-call(f32[4,128,128]{2,1,0:T(8,128)S(1)} %get-tuple-element.22), custom_call_target="InvertDiagBlocksLowerTriangular" | custom-call | tf_op jit(solution)/shard_map/triangular_solve/custom-call.3 | solution.py:77
  247.9 0.8 gather_fusion
  248.9 0.7 fusion.15
  249.7 39.1 %all-gather.3.cloned.1.call-done = bf16[1024,512]{0,1:T(8,128)(2,1)} async-done(((bf16[128,512]{0,1:T(8,128)(2,1)}), bf16[1024,512]{0,1:T(8,128)(2,1)}) %all-gather.3.cloned.1.call-update) | async-done | bytes 1048592 | tf_op jit(solution)/shard_map/all_gather | solution.py:137
  288.8 1.6 fusion
  290.8 1.0 copy-done.3
  292.0 77.6 %all-reduce.6.cloned.1.call-done = f32[512,512]{0,1:T(8,128)} async-done(((f32[512,512]{0,1:T(8,128)}), f32[512,512]{0,1:T(8,128)}) %all-reduce.6.cloned.1.call-update) | async-done | bytes 1048592 | tf_op jit(solution)/shard_map/psum | solution.py:72
  369.6 1.6 copy.16
  371.5 1.0 copy-done.4
  372.5 11.7 %cholesky.358 = f32[128,128]{1,0:T(8,128)S(1)} custom-call(f32[128,128]{1,0:T(8,128)S(1)} %cholesky.439), custom_call_target="Cholesky" | custom-call | tf_op jit(solution)/shard_map/jit(cholesky)/cholesky | solution.py:133
  384.4 9.8 %custom-call.31 = f32[1,128,128]{1,2,0:T(8,128)S(1)} custom-call(f32[1,128,128]{2,1,0:T(8,128)S(1)} %get-tuple-element.63), custom_call_target="InvertDiagBlocksLowerTriangular" | custom-call | tf_op jit(solution)/shard_map/jit(cholesky)/cholesky | solution.py:133
  394.9 11.7 %cholesky.377 = f32[128,128]{1,0:T(8,128)S(1)} custom-call(f32[128,128]{1,0:T(8,128)S(1)} %cholesky.443), custom_call_target="Cholesky" | custom-call | tf_op jit(solution)/shard_map/jit(cholesky)/cholesky | solution.py:133
  406.6 0.7 compare_reduce_fusion.2
  408.0 10.0 %custom-call.32 = f32[1,128,128]{1,2,0:T(8,128)S(1)} custom-call(f32[1,128,128]{2,1,0:T(8,128)S(1)} %get-tuple-element.60), custom_call_target="InvertDiagBlocksLowerTriangular" | custom-call | tf_op jit(solution)/shard_map/jit(cholesky)/cholesky | solution.py:133
  418.7 11.7 %cholesky.398 = f32[128,128]{1,0:T(8,128)S(1)} custom-call(f32[128,128]{1,0:T(8,128)S(1)} %cholesky.448), custom_call_target="Cholesky" | custom-call | tf_op jit(solution)/shard_map/jit(cholesky)/cholesky | solution.py:133
  431.0 9.8 %custom-call.33 = f32[1,128,128]{1,2,0:T(8,128)S(1)} custom-call(f32[1,128,128]{2,1,0:T(8,128)S(1)} %get-tuple-element.57), custom_call_target="InvertDiagBlocksLowerTriangular" | custom-call | tf_op jit(solution)/shard_map/jit(cholesky)/cholesky | solution.py:133
  441.5 11.7 %cholesky.415 = f32[128,128]{1,0:T(8,128)S(1)} custom-call(f32[128,128]{1,0:T(8,128)S(1)} %convolution_subtract_fusion.11), custom_call_target="Cholesky" | custom-call | tf_op jit(solution)/shard_map/jit(cholesky)/cholesky | solution.py:133
  456.9 8.5 %while.5 = (s32[]{:T(128)}, f32[512,512]{1,0:T(8,128)S(1)}, s32[4,2]{0,1:T(2,128)S(1)}, f32[4,128,128]{2,1,0:T(8,128)S(1)}, s32[]{:T(128)}) while((s32[]{:T(128)}, f32[512,512]{1,0:T(8,128)S(1)}, s32[4,2]{0,1:T(2,128)S(1)}, f32[4,128,128]{2,1,0:T(8,128)S(1)}, s32[]{:T(128)}) %tuple.75), condition=%wide.while_cond.clone, body=%wide.while_body.clone.sunk | while | flops 2 | bytes 131181 | solution.py:77
  457.5 1.4 bitcast_dynamic-update-slice_fusion.5
  459.7 1.4 bitcast_dynamic-update-slice_fusion.5
  461.8 1.4 bitcast_dynamic-update-slice_fusion.5
  463.9 1.4 bitcast_dynamic-update-slice_fusion.5
  465.4 39.3 %custom-call.34 = f32[4,128,128]{1,2,0:T(8,128)S(1)} custom-call(f32[4,128,128]{2,1,0:T(8,128)S(1)} %get-tuple-element.23), custom_call_target="InvertDiagBlocksLowerTriangular" | custom-call | tf_op jit(solution)/shard_map/triangular_solve/custom-call.3 | solution.py:77
  506.7 0.8 gather_fusion.1
  507.7 0.7 fusion.17
  508.4 39.1 %all-gather.5.cloned.1.call-done = bf16[1024,512]{0,1:T(8,128)(2,1)} async-done(((bf16[128,512]{0,1:T(8,128)(2,1)}), bf16[1024,512]{0,1:T(8,128)(2,1)}) %all-gather.5.cloned.1.call-update) | async-done | bytes 1048592 | tf_op jit(solution)/shard_map/all_gather | solution.py:137
  547.6 2.4 fusion.3
  (125 shorter events, 20.9 us)
Async XLA Ops:
  6.5 93.7 %all-reduce.4.cloned.1.call-start = ((), (), s32[]{:S(2)}) async-start(), calls=%async_computation | async-start | bytes 2097152 | tf_op jit(solution)/shard_map/psum | solution.py:72
  6.5 10.6 %collective-permute-start = (f32[1,64,512]{2,1,0:T(8,128)}, f32[1,64,512]{2,1,0:T(8,128)S(1)}, u32[]{:S(2)}, u32[]{:S(2)}) collective-permute-start(f32[1,64,512]{2,1,0:T(8,128)} %param.9), channel_id=1, source_target_pairs={{0,4},{1,5},{2,6},{3,7},{4,0},{5,1},{6,2},{7,3},{8,12},{9,13},{10,... | collective-permute-start | bytes 393224 | tf_op jit(solution)/shard_map/ppermute | solution.py:15
  17.6 1.0 copy-start.10
  19.6 1.0 copy-start.2
  20.6 268.2 %all-gather.3.cloned.1.call-start = ((), (), s32[]{:S(2)}) async-start(), calls=%async_computation.1 | async-start | bytes 1179648 | tf_op jit(solution)/shard_map/all_gather | solution.py:137
  100.2 1.7 copy-start
  102.1 1.0 copy-start.6
  103.1 21.7 %copy-start.7 = (f32[512,512]{1,0:T(8,128)S(1)}, f32[512,512]{1,0:T(8,128)}, u32[]{:S(2)}) copy-start(f32[512,512]{1,0:T(8,128)} %copy-done.6) | copy-start | bytes 3145732
  249.6 39.2 %copy-start.8 = (bf16[128,512]{0,1:T(8,128)(2,1)S(1)}, bf16[128,512]{0,1:T(8,128)(2,1)}, u32[]{:S(2)}) copy-start(bf16[128,512]{0,1:T(8,128)(2,1)} %fusion.15) | copy-start | bytes 393220
  249.7 119.9 %all-reduce.6.cloned.1.call-start = ((), (), s32[]{:S(2)}) async-start(), calls=%async_computation.2 | async-start | bytes 2097152 | tf_op jit(solution)/shard_map/psum | solution.py:72
  290.8 1.0 copy-start.3
  291.9 255.7 %all-gather.5.cloned.1.call-start = ((), (), s32[]{:S(2)}) async-start(), calls=%async_computation.3 | async-start | bytes 1179648 | tf_op jit(solution)/shard_map/all_gather | solution.py:137
  369.6 1.7 copy-start.1
  371.5 1.0 copy-start.4
  372.5 21.7 %copy-start.5 = (f32[512,512]{1,0:T(8,128)S(1)}, f32[512,512]{1,0:T(8,128)}, u32[]{:S(2)}) copy-start(f32[512,512]{1,0:T(8,128)} %copy-done.4) | copy-start | bytes 3145732
  508.4 39.2 %copy-start.9 = (bf16[128,512]{0,1:T(8,128)(2,1)S(1)}, bf16[128,512]{0,1:T(8,128)(2,1)}, u32[]{:S(2)}) copy-start(bf16[128,512]{0,1:T(8,128)(2,1)} %fusion.17) | copy-start | bytes 393220
Sparse Core Ops, SparseCore 0:
  20.7 79.4 all-reduce.3
  249.8 38.9 all-gather.2
  292.3 77.2 all-reduce.5
  508.5 38.9 all-gather.4
where the time goes:
time: 567 us; the launch traced here: 557 us
  other arithmetic  251 us (44%)
  waiting for transfers between devices  241 us (43%)
  local copies, waits for them, and re-layouts  28 us (5%)
  between operations  19.6 us (3%)
  matrix products  12.5 us (2%)
    another operation x29, other arithmetic, on_device(): jnp.linalg.cholesky(diag_block)  158 us
    psum x2, waiting for transfers between devices, collect(): result = lax.psum(padded, 'blk')  157 us
    another operation x5, other arithmetic, own_rows(): lax.linalg.triangular_solve(diag_factor, panel_part, left_side=False, low...  90.8 us
    all_gather x2, waiting for transfers between devices, on_device(): lax.all_gather(lowered, 'blk', axis=0, tiled=True)  78.2 us
    another operation x27, local copies, waits for them, and re-layouts, own_rows(): lax.linalg.triangular_solve(diag_factor, panel_part, left_side=False, low...  16.5 us
  transfers between devices with their start and end apart: 5, of which 5 were waited for; matrix products, arithmetic and copies ran while one was open for 0% of the time, Pallas kernels for 0%

commit v1 on v0

--- a/solution.py
+++ b/solution.py
@@ -69,7 +69,9 @@
     padded = lax.dynamic_update_slice(
         padded, jnp.where(is_owner, stacked, 0.0), (0, column_start, 0)
     )
-    result = lax.psum(padded, "blk")
+    result = padded
+    for hop in (1, 2, 4):
+        result = result + lax.ppermute(result, "blk", [(dev, dev ^ hop) for dev in range(8)])
     return result
 
 

time: 567 us -> 591 us (1.042)
  waiting for transfers between devices: 241 us -> 266 us
  starting transfers between devices: 4.19 us -> 13.6 us
    ppermute x0 -> x6, waiting for transfers between devices: none -> 180 us  [collect(): lax.ppermute(result, 'blk', [(dev, dev ^ hop) for dev in range(8)])]
    psum x2 -> x0, waiting for transfers between devices: 157 us -> none  [collect(): result = lax.psum(padded, 'blk')]
    another operation x5, other arithmetic: 90.8 us -> 79 us  [own_rows(): lax.linalg.triangular_solve(diag_factor, panel_part, left_side=False, low...]
    ppermute x0 -> x6, starting transfers between devices: none -> 9.49 us  [collect(): lax.ppermute(result, 'blk', [(dev, dev ^ hop) for dev in range(8)])]
  transfers between devices with their start and end apart: 5 -> 9, of which waited for: 5 -> 9; matrix products, arithmetic and copies ran while one was open for 0% -> 0% of each run, Pallas kernels for 0% -> 0%
where the time goes in v1:
time: 591 us; the launch traced here: 582 us
  waiting for transfers between devices  266 us (45%)
  other arithmetic  246 us (42%)
  local copies, waits for them, and re-layouts  24.4 us (4%)
  between operations  19.3 us (3%)
  starting transfers between devices  13.6 us (2%)
  matrix products  12.5 us (2%)
    ppermute x6, waiting for transfers between devices, collect(): lax.ppermute(result, 'blk', [(dev, dev ^ hop) for dev in range(8)])  180 us
    another operation x29, other arithmetic, on_device(): jnp.linalg.cholesky(diag_block)  159 us
    all_gather x2, waiting for transfers between devices, on_device(): lax.all_gather(lowered, 'blk', axis=0, tiled=True)  80 us
    another operation x5, other arithmetic, own_rows(): lax.linalg.triangular_solve(diag_factor, panel_part, left_side=False, low...  79 us
    another operation x27, local copies, waits for them, and re-layouts, own_rows(): lax.linalg.triangular_solve(diag_factor, panel_part, left_side=False, low...  16.5 us
  transfers between devices with their start and end apart: 9, of which 9 were waited for; matrix products, arithmetic and copies ran while one was open for 0% of the time, Pallas kernels for 0%

profile of v1, /device:TPU:0, one launch (start us, length us, event | category | flops | bytes accessed | tf_op | source)
XLA Modules:
  0.0 581.9 jit_solution(14537322844098712659)
XLA Ops:
  6.5 4.1 collective-permute-start
  11.5 5.7 collective-permute-done
  19.6 1.6 collective-permute-start.1
  21.2 22.8 %collective-permute-done.1 = f32[1,512,512]{1,2,0:T(8,128)S(1)} collective-permute-done((f32[1,512,512]{1,2,0:T(8,128)S(1)}, f32[1,512,512]{1,2,0:T(8,128)S(1)}, u32[]{:S(2)}, u32[]{:S(2)}) %collective-permute-start.1) | collective-permute-done | bytes 1048608 | tf_op jit(solution)/shard_map/ppermute | solution.py:74
  44.0 1.6 collective-permute-start.2
  45.7 22.5 %collective-permute-done.2 = f32[1,512,512]{1,2,0:T(8,128)S(1)} collective-permute-done((f32[1,512,512]{1,2,0:T(8,128)S(1)}, f32[1,512,512]{1,2,0:T(8,128)S(1)}, u32[]{:S(2)}, u32[]{:S(2)}) %collective-permute-start.2) | collective-permute-done | bytes 1048608 | tf_op jit(solution)/shard_map/ppermute | solution.py:74
  68.4 3.3 collective-permute-start.3
  71.8 44.4 %collective-permute-done.3 = f32[1,512,512]{1,2,0:T(8,128)} collective-permute-done((f32[1,512,512]{1,2,0:T(8,128)S(1)}, f32[1,512,512]{1,2,0:T(8,128)}, u32[]{:S(2)}, u32[]{:S(2)}) %collective-permute-start.3) | collective-permute-done | bytes 1048608 | tf_op jit(solution)/shard_map/ppermute | solution.py:74
  116.2 1.4 add_bitcast_fusion.1
  117.6 1.4 copy.13
  119.0 1.9 fusion.6
  120.9 11.7 %cholesky.286 = f32[128,128]{1,0:T(8,128)S(1)} custom-call(f32[128,128]{1,0:T(8,128)S(1)} %cholesky.426), custom_call_target="Cholesky" | custom-call | tf_op jit(solution)/shard_map/jit(cholesky)/cholesky | solution.py:135
  132.8 9.8 %custom-call.27 = f32[1,128,128]{1,2,0:T(8,128)S(1)} custom-call(f32[1,128,128]{2,1,0:T(8,128)S(1)} %get-tuple-element.73), custom_call_target="InvertDiagBlocksLowerTriangular" | custom-call | tf_op jit(solution)/shard_map/jit(cholesky)/cholesky | solution.py:135
  143.3 12.1 %cholesky.305 = f32[128,128]{1,0:T(8,128)S(1)} custom-call(f32[128,128]{1,0:T(8,128)S(1)} %cholesky.430), custom_call_target="Cholesky" | custom-call | tf_op jit(solution)/shard_map/jit(cholesky)/cholesky | solution.py:135
  155.4 9.8 %custom-call.28 = f32[1,128,128]{1,2,0:T(8,128)S(1)} custom-call(f32[1,128,128]{2,1,0:T(8,128)S(1)} %get-tuple-element.70), custom_call_target="InvertDiagBlocksLowerTriangular" | custom-call | tf_op jit(solution)/shard_map/jit(cholesky)/cholesky | solution.py:135
  165.9 11.7 %cholesky.326 = f32[128,128]{1,0:T(8,128)S(1)} custom-call(f32[128,128]{1,0:T(8,128)S(1)} %cholesky.435), custom_call_target="Cholesky" | custom-call | tf_op jit(solution)/shard_map/jit(cholesky)/cholesky | solution.py:135
  178.4 9.8 %custom-call.29 = f32[1,128,128]{1,2,0:T(8,128)S(1)} custom-call(f32[1,128,128]{2,1,0:T(8,128)S(1)} %get-tuple-element.67), custom_call_target="InvertDiagBlocksLowerTriangular" | custom-call | tf_op jit(solution)/shard_map/jit(cholesky)/cholesky | solution.py:135
  188.8 11.9 %cholesky.343 = f32[128,128]{1,0:T(8,128)S(1)} custom-call(f32[128,128]{1,0:T(8,128)S(1)} %slice_subtract_fusion.5), custom_call_target="Cholesky" | custom-call | tf_op jit(solution)/shard_map/jit(cholesky)/cholesky | solution.py:135
  204.8 8.1 %while.4 = (s32[]{:T(128)}, f32[512,512]{1,0:T(8,128)S(1)}, s32[4,2]{0,1:T(2,128)S(1)}, f32[4,128,128]{2,1,0:T(8,128)S(1)}, s32[]{:T(128)}) while((s32[]{:T(128)}, f32[512,512]{1,0:T(8,128)S(1)}, s32[4,2]{0,1:T(2,128)S(1)}, f32[4,128,128]{2,1,0:T(8,128)S(1)}, s32[]{:T(128)}) %tuple.61), condition=%wide.while_cond, body=%wide.while_body.sunk | while | flops 2 | bytes 131181 | solution.py:79
  205.5 1.3 bitcast_dynamic-update-slice_fusion.4
  207.5 1.3 bitcast_dynamic-update-slice_fusion.4
  209.6 1.3 bitcast_dynamic-update-slice_fusion.4
  211.6 1.3 bitcast_dynamic-update-slice_fusion.4
  213.0 39.3 %custom-call.30 = f32[4,128,128]{1,2,0:T(8,128)S(1)} custom-call(f32[4,128,128]{2,1,0:T(8,128)S(1)} %get-tuple-element.22), custom_call_target="InvertDiagBlocksLowerTriangular" | custom-call | tf_op jit(solution)/shard_map/triangular_solve/custom-call.3 | solution.py:79
  256.1 40.7 %all-gather.3.cloned.1.call-done = bf16[1024,512]{0,1:T(8,128)(2,1)} async-done(((bf16[128,512]{0,1:T(8,128)(2,1)}), bf16[1024,512]{0,1:T(8,128)(2,1)}) %all-gather.3.cloned.1.call-update) | async-done | bytes 1048592 | tf_op jit(solution)/shard_map/all_gather | solution.py:139
  296.8 1.6 fusion
  298.8 1.1 collective-permute-start.4
  299.9 23.1 %collective-permute-done.4 = f32[1,512,512]{1,2,0:T(8,128)S(1)} collective-permute-done((f32[1,512,512]{1,2,0:T(8,128)S(1)}, f32[1,512,512]{1,2,0:T(8,128)S(1)}, u32[]{:S(2)}, u32[]{:S(2)}) %collective-permute-start.4) | collective-permute-done | bytes 1048608 | tf_op jit(solution)/shard_map/ppermute | solution.py:74
  323.2 23.3 %collective-permute-done.5 = f32[1,512,512]{1,2,0:T(8,128)S(1)} collective-permute-done((f32[1,512,512]{1,2,0:T(8,128)S(1)}, f32[1,512,512]{1,2,0:T(8,128)S(1)}, u32[]{:S(2)}, u32[]{:S(2)}) %collective-permute-start.5) | collective-permute-done | bytes 1048608 | tf_op jit(solution)/shard_map/ppermute | solution.py:74
  346.7 1.7 collective-permute-start.6
  348.5 44.1 %collective-permute-done.6 = f32[1,512,512]{1,2,0:T(8,128)S(1)} collective-permute-done((f32[1,512,512]{1,2,0:T(8,128)S(1)}, f32[1,512,512]{1,2,0:T(8,128)S(1)}, u32[]{:S(2)}, u32[]{:S(2)}) %collective-permute-start.6) | collective-permute-done | bytes 1048608 | tf_op jit(solution)/shard_map/ppermute | solution.py:74
  393.8 1.3 copy.16
  395.2 1.9 fusion.5
  397.1 11.7 %cholesky.358 = f32[128,128]{1,0:T(8,128)S(1)} custom-call(f32[128,128]{1,0:T(8,128)S(1)} %cholesky.439), custom_call_target="Cholesky" | custom-call | tf_op jit(solution)/shard_map/jit(cholesky)/cholesky | solution.py:135
  409.0 9.8 %custom-call.31 = f32[1,128,128]{1,2,0:T(8,128)S(1)} custom-call(f32[1,128,128]{2,1,0:T(8,128)S(1)} %get-tuple-element.63), custom_call_target="InvertDiagBlocksLowerTriangular" | custom-call | tf_op jit(solution)/shard_map/jit(cholesky)/cholesky | solution.py:135
  419.4 12.1 %cholesky.377 = f32[128,128]{1,0:T(8,128)S(1)} custom-call(f32[128,128]{1,0:T(8,128)S(1)} %cholesky.443), custom_call_target="Cholesky" | custom-call | tf_op jit(solution)/shard_map/jit(cholesky)/cholesky | solution.py:135
  432.9 9.8 %custom-call.32 = f32[1,128,128]{1,2,0:T(8,128)S(1)} custom-call(f32[1,128,128]{2,1,0:T(8,128)S(1)} %get-tuple-element.60), custom_call_target="InvertDiagBlocksLowerTriangular" | custom-call | tf_op jit(solution)/shard_map/jit(cholesky)/cholesky | solution.py:135
  443.4 11.7 %cholesky.398 = f32[128,128]{1,0:T(8,128)S(1)} custom-call(f32[128,128]{1,0:T(8,128)S(1)} %cholesky.448), custom_call_target="Cholesky" | custom-call | tf_op jit(solution)/shard_map/jit(cholesky)/cholesky | solution.py:135
  455.8 9.8 %custom-call.33 = f32[1,128,128]{1,2,0:T(8,128)S(1)} custom-call(f32[1,128,128]{2,1,0:T(8,128)S(1)} %get-tuple-element.57), custom_call_target="InvertDiagBlocksLowerTriangular" | custom-call | tf_op jit(solution)/shard_map/jit(cholesky)/cholesky | solution.py:135
  466.2 11.9 %cholesky.415 = f32[128,128]{1,0:T(8,128)S(1)} custom-call(f32[128,128]{1,0:T(8,128)S(1)} %slice_subtract_fusion.4), custom_call_target="Cholesky" | custom-call | tf_op jit(solution)/shard_map/jit(cholesky)/cholesky | solution.py:135
  481.5 8.5 %while.5 = (s32[]{:T(128)}, f32[512,512]{1,0:T(8,128)S(1)}, s32[4,2]{0,1:T(2,128)S(1)}, f32[4,128,128]{2,1,0:T(8,128)S(1)}, s32[]{:T(128)}) while((s32[]{:T(128)}, f32[512,512]{1,0:T(8,128)S(1)}, s32[4,2]{0,1:T(2,128)S(1)}, f32[4,128,128]{2,1,0:T(8,128)S(1)}, s32[]{:T(128)}) %tuple.71), condition=%wide.while_cond.clone, body=%wide.while_body.clone.sunk | while | flops 2 | bytes 131181 | solution.py:79
  482.2 1.4 bitcast_dynamic-update-slice_fusion.5
  484.3 1.4 bitcast_dynamic-update-slice_fusion.5
  486.5 1.4 bitcast_dynamic-update-slice_fusion.5
  488.6 1.4 bitcast_dynamic-update-slice_fusion.5
  490.0 39.3 %custom-call.34 = f32[4,128,128]{1,2,0:T(8,128)S(1)} custom-call(f32[4,128,128]{2,1,0:T(8,128)S(1)} %get-tuple-element.23), custom_call_target="InvertDiagBlocksLowerTriangular" | custom-call | tf_op jit(solution)/shard_map/triangular_solve/custom-call.3 | solution.py:79
  533.1 39.3 %all-gather.5.cloned.1.call-done = bf16[1024,512]{0,1:T(8,128)(2,1)} async-done(((bf16[128,512]{0,1:T(8,128)(2,1)}), bf16[1024,512]{0,1:T(8,128)(2,1)}) %all-gather.5.cloned.1.call-update) | async-done | bytes 1048592 | tf_op jit(solution)/shard_map/all_gather | solution.py:139
  572.4 2.4 fusion.3
  (123 shorter events, 27.7 us)
Async XLA Ops:
  6.5 290.2 %all-gather.3.cloned.1.call-start = ((), (), s32[]{:S(2)}) async-start(), calls=%async_computation | async-start | bytes 1179648 | tf_op jit(solution)/shard_map/all_gather | solution.py:139
  6.5 10.6 %collective-permute-start = (f32[1,64,512]{2,1,0:T(8,128)}, f32[1,64,512]{2,1,0:T(8,128)S(1)}, u32[]{:S(2)}, u32[]{:S(2)}) collective-permute-start(f32[1,64,512]{2,1,0:T(8,128)} %param.9), channel_id=1, source_target_pairs={{0,4},{1,5},{2,6},{3,7},{4,0},{5,1},{6,2},{7,3},{8,12},{9,13},{10,... | collective-permute-start | bytes 393224 | tf_op jit(solution)/shard_map/ppermute | solution.py:15
  17.6 1.0 copy-start.3
  19.6 24.4 %collective-permute-start.1 = (f32[1,512,512]{1,2,0:T(8,128)S(1)}, f32[1,512,512]{1,2,0:T(8,128)S(1)}, u32[]{:S(2)}, u32[]{:S(2)}) collective-permute-start(f32[1,512,512]{1,2,0:T(8,128)S(1)} %constant_dynamic-update-slice_fusion.3), channel_id=1, source_target_pairs={{0,1},{1,0},{2,3},{3,2},{4,5},{5,4},{6,7},{7,6},{8,9},{9,8},{10,11... | collective-permute-start | bytes 3145736 | tf_op jit(solution)/shard_map/ppermute | solution.py:74
  44.0 24.1 %collective-permute-start.2 = (f32[1,512,512]{1,2,0:T(8,128)S(1)}, f32[1,512,512]{1,2,0:T(8,128)S(1)}, u32[]{:S(2)}, u32[]{:S(2)}) collective-permute-start(f32[1,512,512]{1,2,0:T(8,128)S(1)} %add_dynamic-update-slice_fusion.1), channel_id=1, source_target_pairs={{0,2},{1,3},{2,0},{3,1},{4,6},{5,7},{6,4},{7,5},{8,10},{9,11},{10,... | collective-permute-start | bytes 3145736 | tf_op jit(solution)/shard_map/ppermute | solution.py:74
  68.4 47.8 %collective-permute-start.3 = (f32[1,512,512]{1,2,0:T(8,128)S(1)}, f32[1,512,512]{1,2,0:T(8,128)}, u32[]{:S(2)}, u32[]{:S(2)}) collective-permute-start(f32[1,512,512]{1,2,0:T(8,128)S(1)} %add.213), channel_id=1, source_target_pairs={{0,4},{1,5},{2,6},{3,7},{4,0},{5,1},{6,2},{7,3},{8,12},{9,13},{10,... | collective-permute-start | bytes 3145736 | tf_op jit(solution)/shard_map/ppermute | solution.py:74
  256.0 40.8 %copy-start.1 = (bf16[128,512]{0,1:T(8,128)(2,1)S(1)}, bf16[128,512]{0,1:T(8,128)(2,1)}, u32[]{:S(2)}) copy-start(bf16[128,512]{0,1:T(8,128)(2,1)} %fusion.17) | copy-start | bytes 393220
  256.0 316.4 %all-gather.5.cloned.1.call-start = ((), (), s32[]{:S(2)}) async-start(), calls=%async_computation.1 | async-start | bytes 1179648 | tf_op jit(solution)/shard_map/all_gather | solution.py:139
  298.8 24.2 %collective-permute-start.4 = (f32[1,512,512]{1,2,0:T(8,128)S(1)}, f32[1,512,512]{1,2,0:T(8,128)S(1)}, u32[]{:S(2)}, u32[]{:S(2)}) collective-permute-start(f32[1,512,512]{1,2,0:T(8,128)S(1)} %constant_dynamic-update-slice_fusion.2), channel_id=1, source_target_pairs={{0,1},{1,0},{2,3},{3,2},{4,5},{5,4},{6,7},{7,6},{8,9},{9,8},{10,11... | collective-permute-start | bytes 3145736 | tf_op jit(solution)/shard_map/ppermute | solution.py:74
  323.1 23.4 %collective-permute-start.5 = (f32[1,512,512]{1,2,0:T(8,128)S(1)}, f32[1,512,512]{1,2,0:T(8,128)S(1)}, u32[]{:S(2)}, u32[]{:S(2)}) collective-permute-start(f32[1,512,512]{1,2,0:T(8,128)S(1)} %add_dynamic-update-slice_fusion), channel_id=1, source_target_pairs={{0,2},{1,3},{2,0},{3,1},{4,6},{5,7},{6,4},{7,5},{8,10},{9,11},{10,... | collective-permute-start | bytes 3145736 | tf_op jit(solution)/shard_map/ppermute | solution.py:74
  346.7 45.9 %collective-permute-start.6 = (f32[1,512,512]{1,2,0:T(8,128)S(1)}, f32[1,512,512]{1,2,0:T(8,128)S(1)}, u32[]{:S(2)}, u32[]{:S(2)}) collective-permute-start(f32[1,512,512]{1,2,0:T(8,128)S(1)} %add.217), channel_id=1, source_target_pairs={{0,4},{1,5},{2,6},{3,7},{4,0},{5,1},{6,2},{7,3},{8,12},{9,13},{10,... | collective-permute-start | bytes 3145736 | tf_op jit(solution)/shard_map/ppermute | solution.py:74
  392.6 1.0 copy-start
  533.0 39.4 %copy-start.2 = (bf16[128,512]{0,1:T(8,128)(2,1)S(1)}, bf16[128,512]{0,1:T(8,128)(2,1)}, u32[]{:S(2)}) copy-start(bf16[128,512]{0,1:T(8,128)(2,1)} %fusion.19) | copy-start | bytes 393220
Sparse Core Ops, SparseCore 0:
  256.1 40.5 all-gather.2
  533.2 39.1 all-gather.4
